TPU v7x, 512 devices: a whole 4x4x16 slice. The times are simulated.
512 devices in a mesh: gx: 8 (over x, core), gy: 4 (over y), gz: 16 (over z).
Axes of the slice: x: 4, y: 4, z: 16, core: 2. Of those that a mesh axis runs over, the one named last changes fastest.
Arguments:
- residual: bfloat16 [8, 4, 16, 3, 256, 256], P('gx', 'gy', 'gz'), may hold values from -6 to 6
- face_basis: bfloat16 [8, 4, 16, 3, 256, 256], P('gx', 'gy', 'gz'), may hold values from -0.375 to 0.375
- factor: bfloat16 [8, 4, 16, 768, 768], P('gx', 'gy', 'gz'), may hold values from -0.21875 to 0.21875
- coarse_inv: bfloat16 [8, 4, 16, 768, 768], P('gx', 'gy', 'gz'), may hold values from -0.21875 to 0.21875
- item_owner: int32 [8, 4, 16, 24], P('gx', 'gy', 'gz'), may hold values from 0 to 15, as said below
Outputs:
- result: bfloat16 [8, 4, 16, 3, 256, 256], P('gx', 'gy', 'gz')
Inputs may be any that keep to these rules, and one draw needn't show every extreme that they name: `item_owner`: within the groups of one subdomain, at most 3 name the same owner, and in every subdomain some owner is named exactly 3 times.
All inputs are finite; a program needn't handle non-finite values.
Results may differ from a plain program's by a relative error of at most 0.006.
Values may be sent and summed in bfloat16 or wider, within the bound.
A program may use at most 64 MiB of HBM per device.

v0:
```python
import jax
import jax.numpy as jnp
from jax import lax
from jax.sharding import PartitionSpec as P

PF = 128
GROUP = 16
ITEMS = 24


def shifted(block, axis, distance):
    devices = range(lax.axis_size(axis))
    route = [((i - distance) % len(devices), i) for i in devices]
    return lax.ppermute(block, axis, route)


def along_axes(faces, offset):
    from_x = shifted(faces[0], "gx", offset)
    from_y = shifted(faces[1], "gy", offset)
    from_z = shifted(faces[2], "gz", offset)
    return jnp.stack([from_x, from_y, from_z])


def apply_coarse(matrix, block):
    rows = block.shape[3]
    stacked = block.reshape(-1, rows)
    answer = lax.dot_general(
        matrix, stacked, (((0,), (0,)), ((), ())), preferred_element_type=jnp.float32
    )
    return answer.astype(jnp.bfloat16).reshape(block.shape)


def rank_within(owners):
    item_index = jnp.arange(owners.shape[-1], dtype=jnp.int32)
    same_owner = owners[..., :, None] == owners[..., None, :]
    earlier = item_index[:, None] > item_index[None, :]
    return jnp.sum((same_owner & earlier).astype(jnp.int32), axis=-1)


def body(residual, face_basis, factor, coarse_inv, item_owner):
    local_resid = residual[0, 0, 0]
    local_basis = face_basis[0, 0, 0]
    local_factor = factor[0, 0, 0]
    local_coarse = coarse_inv[0, 0, 0]
    owners = item_owner[0, 0, 0]
    columns = local_resid.shape[-1]
    column_size = lax.axis_size("gz")
    send_cap = local_coarse.shape[0] // (column_size * GROUP)
    transformed = jnp.einsum(
        "fac,far->fcr", local_basis, local_resid, preferred_element_type=jnp.float32
    )
    primal_items = transformed[:, :PF, :].astype(jnp.bfloat16).reshape(ITEMS, GROUP, columns)
    dual_own = transformed[:, PF:, :].astype(jnp.bfloat16)
    slot_rank = rank_within(owners)
    send_slot = owners * send_cap + slot_rank
    dual_in = along_axes(dual_own, 1)
    dual_load = (jnp.concatenate([dual_in, dual_own], axis=0) * 0.5).reshape(-1, columns)
    half_solve = lax.dot_general(
        local_factor, dual_load, (((0,), (0,)), ((), ())), preferred_element_type=jnp.float32
    ).astype(jnp.bfloat16)
    solved = (
        jnp.dot(local_factor, half_solve, preferred_element_type=jnp.float32)
        .astype(jnp.bfloat16)
        .reshape(6, -1, columns)
    )
    from_above = along_axes(solved[:3], -1)
    dual_part = (0.5 * (solved[3:].astype(jnp.float32) + from_above.astype(jnp.float32))).astype(
        jnp.bfloat16
    )
    outgoing = jnp.zeros((column_size * send_cap, GROUP, columns), jnp.bfloat16)
    outgoing = (
        outgoing.at[send_slot].set(primal_items).reshape(column_size, send_cap, GROUP, columns)
    )
    answer = apply_coarse(
        local_coarse, lax.all_to_all(outgoing, "gz", split_axis=0, concat_axis=0, tiled=True)
    )
    returned = lax.all_to_all(answer, "gz", split_axis=0, concat_axis=0, tiled=True)
    flat_back = returned.reshape(column_size * send_cap, GROUP, columns)
    primal_part = jnp.take(flat_back, send_slot, axis=0).reshape(3, PF, columns)
    combined = jnp.concatenate([primal_part, dual_part], axis=1)
    result = jnp.einsum("fac,fcr->far", local_basis, combined, preferred_element_type=jnp.float32)
    return result.astype(jnp.bfloat16)[None, None, None]


def solution(mesh):
    in_specs = (
        P("gx", "gy", "gz", None, None, None),
        P("gx", "gy", "gz", None, None, None),
        P("gx", "gy", "gz", None, None),
        P("gx", "gy", "gz", None, None),
        P("gx", "gy", "gz", None),
    )
    out_specs = P("gx", "gy", "gz", None, None, None)
    return jax.shard_map(body, mesh=mesh, in_specs=in_specs, out_specs=out_specs, check_vma=False)
```

profile of v0, /device:TPU:6, one launch (start us, length us, event | category | flops | bytes accessed | tf_op | source)
XLA Modules:
  0.0 77.9 jit_solution(8283784142092098555)
XLA Ops:
  0.0 0.0 copy-start
  0.0 0.0 copy-start.2
  0.0 1.5 %convolution_convert_fusion.4 = bf16[3,256,256]{2,1,0:T(8,128)(2,1)S(1)} fusion(bf16[1,1,1,3,256,256]{5,4,3,2,1,0:T(8,128)(2,1)} %param.5, bf16[1,1,1,3,256,256]{5,4,3,2,1,0:T(8,128)(2,1)} %param.6), kind=kOutput, calls=%fused_computation.6 | convolution fusion | flops 100859904 | bytes 1179648 | tf_op jit(solution)/shard_map/fac,far->fcr/dot_general | solution.py:49
  1.6 0.0 copy-done.2
  1.6 0.2 convert_reduce_fusion
  1.8 0.8 broadcast_in_dim.26
  2.5 3.9 %scatter_fusion = bf16[48,16,256]{2,1,0:T(8,128)(2,1)} fusion(bf16[48,16,256]{2,1,0:T(8,128)(2,1)} %broadcast_in_dim.26, s32[24]{0:T(128)S(1)} %fusion.13, bf16[24,16,256]{2,1,0:T(8,128)(2,1)S(1)} %bitcast.57), kind=kCustom, calls=%fused_computation.1 | custom fusion | bytes 589920 | tf_op jit(solution)/shard_map/scatter | solution.py:72
  6.4 15.2 %all-to-all-start = ((bf16[16,3,16,256]{3,2,1,0:T(8,128)(2,1)}), bf16[16,3,16,256]{3,2,1,0:T(8,128)(2,1)S(1)}, u32[]{:S(2)}, u32[]{:S(2)}) async-start(bf16[16,3,16,256]{3,2,1,0:T(8,128)(2,1)} %bitcast.7), calls=%async_computation | async-start | bytes 786432 | tf_op jit(solution)/shard_map/all_to_all | solution.py:75
  21.7 0.0 collective-permute-start
  21.7 3.5 %collective-permute-start.1 = (bf16[128,256]{1,0:T(8,128)(2,1)S(1)}, bf16[128,256]{1,0:T(8,128)(2,1)S(1)}, u32[]{:S(2)}, u32[]{:S(2)}) collective-permute-start(bf16[128,256]{1,0:T(8,128)(2,1)S(1)} %get-tuple-element.12), channel_id=1, source_target_pairs={{48,0},{0,16},{16,32},{32,48},{49,1},{1,17},{17,33},{33,49},{50,2}... | collective-permute-start | bytes 196616 | tf_op jit(solution)/shard_map/ppermute | solution.py:14
  25.2 3.8 %collective-permute-start.2 = (bf16[128,256]{1,0:T(8,128)(2,1)S(1)}, bf16[128,256]{1,0:T(8,128)(2,1)S(1)}, u32[]{:S(2)}, u32[]{:S(2)}) collective-permute-start(bf16[128,256]{1,0:T(8,128)(2,1)S(1)} %get-tuple-element.11), channel_id=1, source_target_pairs={{15,0},{0,1},{1,2},{2,3},{3,4},{4,5},{5,6},{6,7},{7,8},{8,9},{9,10... | collective-permute-start | bytes 196616 | tf_op jit(solution)/shard_map/ppermute | solution.py:14
  29.0 18.4 %all-to-all-done = bf16[16,3,16,256]{3,2,1,0:T(8,128)(2,1)S(1)} async-done(((bf16[16,3,16,256]{3,2,1,0:T(8,128)(2,1)}), bf16[16,3,16,256]{3,2,1,0:T(8,128)(2,1)S(1)}, u32[]{:S(2)}, u32[]{:S(2)}) %all-to-all-start) | async-done | bytes 393248 | tf_op jit(solution)/shard_map/all_to_all | solution.py:75
  47.4 0.0 copy-done
  47.4 0.5 fusion.1
  47.9 0.9 %copy.15 = bf16[768,256]{1,0:T(8,128)(2,1)} copy(bf16[768,256]{0,1:T(8,128)(2,1)S(1)} %fusion.1) | data formatting | bytes 786432 | tf_op jit(solution)/shard_map/convert_element_type | solution.py:30
  48.8 4.5 %all-to-all-start.1 = ((bf16[16,3,16,256]{3,2,1,0:T(8,128)(2,1)}), bf16[16,3,16,256]{3,2,1,0:T(8,128)(2,1)S(1)}, u32[]{:S(2)}, u32[]{:S(2)}) async-start(bf16[16,3,16,256]{3,2,1,0:T(8,128)(2,1)} %bitcast.11), calls=%async_computation.1 | async-start | bytes 786432 | tf_op jit(solution)/shard_map/all_to_all | solution.py:77
  53.4 0.1 reduce_sum.14
  53.5 0.1 mul.42
  53.6 0.1 broadcast_in_dim.23
  53.6 0.1 broadcast_in_dim.24
  53.7 0.0 collective-permute-done
  53.7 0.0 collective-permute-done.1
  53.8 0.0 collective-permute-done.2
  53.8 0.1 maximum_multiply_fusion
  53.8 2.8 %fusion.2 = bf16[768,256]{0,1:T(8,128)(2,1)S(1)} fusion(bf16[768,256]{1,0:T(8,128)(2,1)S(1)} %bitcast.59, bf16[1,1,1,768,768]{4,3,2,1,0:T(8,128)(2,1)} %param.7), kind=kOutput, calls=%fused_computation.9 | convolution fusion | flops 604372992 | bytes 1966080 | tf_op jit(solution)/shard_map/dot_general | solution.py:62
  56.7 0.0 collective-permute-start.3
  56.7 4.9 %collective-permute-start.4 = (bf16[128,256]{0,1:T(8,128)(2,1)S(1)}, bf16[128,256]{0,1:T(8,128)(2,1)S(1)}, u32[]{:S(2)}, u32[]{:S(2)}) collective-permute-start(bf16[128,256]{0,1:T(8,128)(2,1)S(1)} %get-tuple-element.9), channel_id=1, source_target_pairs={{16,0},{32,16},{48,32},{0,48},{17,1},{33,17},{49,33},{1,49},{18,2}... | collective-permute-start | bytes 196616 | tf_op jit(solution)/shard_map/ppermute | solution.py:14
  61.6 5.1 %collective-permute-start.5 = (bf16[128,256]{0,1:T(8,128)(2,1)S(1)}, bf16[128,256]{0,1:T(8,128)(2,1)S(1)}, u32[]{:S(2)}, u32[]{:S(2)}) collective-permute-start(bf16[128,256]{0,1:T(8,128)(2,1)S(1)} %get-tuple-element.8), channel_id=1, source_target_pairs={{1,0},{2,1},{3,2},{4,3},{5,4},{6,5},{7,6},{8,7},{9,8},{10,9},{11,1... | collective-permute-start | bytes 196616 | tf_op jit(solution)/shard_map/ppermute | solution.py:14
  66.7 0.2 copy.17
  66.9 0.2 copy.18
  67.1 0.0 copy-start.1
  67.1 0.0 collective-permute-done.3
  67.1 0.0 collective-permute-done.4
  67.1 5.7 %collective-permute-done.5 = bf16[128,256]{0,1:T(8,128)(2,1)S(1)} collective-permute-done((bf16[128,256]{0,1:T(8,128)(2,1)S(1)}, bf16[128,256]{0,1:T(8,128)(2,1)S(1)}, u32[]{:S(2)}, u32[]{:S(2)}) %collective-permute-start.5) | collective-permute-done | bytes 65568 | tf_op jit(solution)/shard_map/ppermute | solution.py:14
  72.8 0.1 multiply_convert_fusion
  72.8 3.1 %all-to-all-done.1 = bf16[16,3,16,256]{3,2,1,0:T(8,128)(2,1)S(1)} async-done(((bf16[16,3,16,256]{3,2,1,0:T(8,128)(2,1)}), bf16[16,3,16,256]{3,2,1,0:T(8,128)(2,1)S(1)}, u32[]{:S(2)}, u32[]{:S(2)}) %all-to-all-start.1) | async-done | bytes 393248 | tf_op jit(solution)/shard_map/all_to_all | solution.py:77
  75.9 0.6 gather_fusion
  76.5 0.2 copy.16
  76.7 0.0 copy-done.1
  76.7 0.3 fusion
  77.0 0.9 %copy.19 = bf16[1,1,1,3,256,256]{5,4,3,2,1,0:T(8,128)(2,1)} copy(bf16[1,1,1,3,256,256]{4,5,3,2,1,0:T(8,128)(2,1)S(1)} %fusion) | data formatting | bytes 786432 | tf_op jit(solution)/shard_map/broadcast_in_dim | solution.py:82
  (9 shorter events, 0.2 us)
Async XLA Ops:
  0.0 47.4 %copy-start = (bf16[1,1,1,768,768]{4,3,2,1,0:T(8,128)(2,1)S(1)}, bf16[1,1,1,768,768]{4,3,2,1,0:T(8,128)(2,1)}, u32[]{:S(2)}) copy-start(bf16[1,1,1,768,768]{4,3,2,1,0:T(8,128)(2,1)} %param.8) | copy-start | bytes 3538948
  0.0 1.6 %copy-start.2 = (s32[1,1,1,24]{3,2,1,0:T(1,128)S(1)}, s32[1,1,1,24]{3,2,1,0:T(1,128)}, u32[]{:S(2)}) copy-start(s32[1,1,1,24]{3,2,1,0:T(1,128)} %param.9) | copy-start | bytes 292
  6.4 41.0 %all-to-all-start = ((bf16[16,3,16,256]{3,2,1,0:T(8,128)(2,1)}), bf16[16,3,16,256]{3,2,1,0:T(8,128)(2,1)S(1)}, u32[]{:S(2)}, u32[]{:S(2)}) async-start(bf16[16,3,16,256]{3,2,1,0:T(8,128)(2,1)} %bitcast.7), calls=%async_computation | async-start | bytes 786432 | tf_op jit(solution)/shard_map/all_to_all | solution.py:75
  21.7 32.1 %collective-permute-start = (bf16[128,256]{1,0:T(8,128)(2,1)S(1)}, bf16[128,256]{1,0:T(8,128)(2,1)S(1)}, u32[]{:S(2)}, u32[]{:S(2)}) collective-permute-start(bf16[128,256]{1,0:T(8,128)(2,1)S(1)} %get-tuple-element.10), channel_id=1, source_target_pairs={{448,0},{0,64},{64,128},{128,192},{192,256},{256,320},{320,384},{3... | collective-permute-start | bytes 196616 | tf_op jit(solution)/shard_map/ppermute | solution.py:14
  21.7 32.1 %collective-permute-start.1 = (bf16[128,256]{1,0:T(8,128)(2,1)S(1)}, bf16[128,256]{1,0:T(8,128)(2,1)S(1)}, u32[]{:S(2)}, u32[]{:S(2)}) collective-permute-start(bf16[128,256]{1,0:T(8,128)(2,1)S(1)} %get-tuple-element.12), channel_id=1, source_target_pairs={{48,0},{0,16},{16,32},{32,48},{49,1},{1,17},{17,33},{33,49},{50,2}... | collective-permute-start | bytes 196616 | tf_op jit(solution)/shard_map/ppermute | solution.py:14
  25.2 28.6 %collective-permute-start.2 = (bf16[128,256]{1,0:T(8,128)(2,1)S(1)}, bf16[128,256]{1,0:T(8,128)(2,1)S(1)}, u32[]{:S(2)}, u32[]{:S(2)}) collective-permute-start(bf16[128,256]{1,0:T(8,128)(2,1)S(1)} %get-tuple-element.11), channel_id=1, source_target_pairs={{15,0},{0,1},{1,2},{2,3},{3,4},{4,5},{5,6},{6,7},{7,8},{8,9},{9,10... | collective-permute-start | bytes 196616 | tf_op jit(solution)/shard_map/ppermute | solution.py:14
  48.8 27.1 %all-to-all-start.1 = ((bf16[16,3,16,256]{3,2,1,0:T(8,128)(2,1)}), bf16[16,3,16,256]{3,2,1,0:T(8,128)(2,1)S(1)}, u32[]{:S(2)}, u32[]{:S(2)}) async-start(bf16[16,3,16,256]{3,2,1,0:T(8,128)(2,1)} %bitcast.11), calls=%async_computation.1 | async-start | bytes 786432 | tf_op jit(solution)/shard_map/all_to_all | solution.py:77
  56.7 10.4 %collective-permute-start.3 = (bf16[128,256]{0,1:T(8,128)(2,1)S(1)}, bf16[128,256]{0,1:T(8,128)(2,1)S(1)}, u32[]{:S(2)}, u32[]{:S(2)}) collective-permute-start(bf16[128,256]{0,1:T(8,128)(2,1)S(1)} %get-tuple-element.7), channel_id=1, source_target_pairs={{64,0},{128,64},{192,128},{256,192},{320,256},{384,320},{448,384},... | collective-permute-start | bytes 196616 | tf_op jit(solution)/shard_map/ppermute | solution.py:14
  56.7 10.4 %collective-permute-start.4 = (bf16[128,256]{0,1:T(8,128)(2,1)S(1)}, bf16[128,256]{0,1:T(8,128)(2,1)S(1)}, u32[]{:S(2)}, u32[]{:S(2)}) collective-permute-start(bf16[128,256]{0,1:T(8,128)(2,1)S(1)} %get-tuple-element.9), channel_id=1, source_target_pairs={{16,0},{32,16},{48,32},{0,48},{17,1},{33,17},{49,33},{1,49},{18,2}... | collective-permute-start | bytes 196616 | tf_op jit(solution)/shard_map/ppermute | solution.py:14
  61.6 11.1 %collective-permute-start.5 = (bf16[128,256]{0,1:T(8,128)(2,1)S(1)}, bf16[128,256]{0,1:T(8,128)(2,1)S(1)}, u32[]{:S(2)}, u32[]{:S(2)}) collective-permute-start(bf16[128,256]{0,1:T(8,128)(2,1)S(1)} %get-tuple-element.8), channel_id=1, source_target_pairs={{1,0},{2,1},{3,2},{4,3},{5,4},{6,5},{7,6},{8,7},{9,8},{10,9},{11,1... | collective-permute-start | bytes 196616 | tf_op jit(solution)/shard_map/ppermute | solution.py:14
  67.1 9.6 %copy-start.1 = (bf16[1,1,1,3,256,256]{5,4,3,2,1,0:T(8,128)(2,1)S(1)}, bf16[1,1,1,3,256,256]{5,4,3,2,1,0:T(8,128)(2,1)}, u32[]{:S(2)}) copy-start(bf16[1,1,1,3,256,256]{5,4,3,2,1,0:T(8,128)(2,1)} %param.6) | copy-start | bytes 1179652
where the time goes:
time: 78.6 us; the launch traced here: 77.9 us
  starting transfers between devices  37 us (47%)
  waiting for transfers between devices  27.1 us (34%)
  local copies, waits for them, and re-layouts  7.96 us (10%)
  matrix products  5.16 us (7%)
    all_to_all x1, waiting for transfers between devices, body(): lax.all_to_all(outgoing, 'gz', split_axis=0, concat_axis=0, tiled=True)  18.4 us
    ppermute x6, starting transfers between devices, shifted(): return lax.ppermute(block, axis, route)  17.3 us
    all_to_all x1, starting transfers between devices, body(): lax.all_to_all(outgoing, 'gz', split_axis=0, concat_axis=0, tiled=True)  15.2 us
    ppermute x6, waiting for transfers between devices, shifted(): return lax.ppermute(block, axis, route)  5.67 us
    all_to_all x1, starting transfers between devices, body(): lax.all_to_all(answer, 'gz', split_axis=0, concat_axis=0, tiled=True)  4.51 us
    scatter x1, local copies, waits for them, and re-layouts, body(): outgoing.at[send_slot].set(primal_items)  3.88 us
    all_to_all x1, waiting for transfers between devices, body(): lax.all_to_all(answer, 'gz', split_axis=0, concat_axis=0, tiled=True)  3.08 us
    dot_general x1, matrix products, body(): jnp.dot(local_factor, half_solve, preferred_element_type=jnp.float32)  2.82 us
  transfers between devices with their start and end apart: 8, of which 3 were waited for; matrix products, arithmetic and copies ran while one was open for 7% of the time, Pallas kernels for 0%

commit v1 on v0

v1 whole, which is shorter than its diff:
```python
import functools

import jax
import jax.numpy as jnp
from jax import lax
from jax.experimental import pallas as pl
from jax.experimental.pallas import tpu as pltpu
from jax.sharding import PartitionSpec as P

MESH = pl.DeviceIdType.MESH
PF = 128
GROUP = 16
ITEMS = 24
CAP = 3
NZ = 16
LANES = 128
BLOCK = CAP * GROUP
REACH = 4
DIRECT = 4

FAR = [(8, 0)] + [(d, s) for d in range(7, DIRECT, -1) for s in (1, -1)]
NEAR = [(d, s) for d in range(DIRECT, 0, -1) for s in (1, -1)]
ROUTES = FAR + NEAR

STEPS = (
    "slots",
    "primal0",
    "pack0",
    "barrier",
    "F0far",
    "F0near",
    "keep0",
    "dual",
    "up",
    "primal1",
    "pack1",
    "F1far",
    "keep1",
    "spread",
    "F0fwd",
    "F1near",
    "solve",
    "down",
    "ctrans",
    "F1fwd",
    "coarse0",
    "B0far",
    "B0near",
    "mean",
    "coarse1",
    "B1far",
    "B0fwd",
    "B1n43",
    "B1fwd",
    "B1n21",
    "final0",
    "final1",
)


def mod(value, n):
    return lax.rem(value + 4 * n, n)


def dot(a, b):
    return jnp.dot(a, b, preferred_element_type=jnp.float32)


def dot_nt(a, b):
    return lax.dot_general(a, b, (((1,), (1,)), ((), ())), preferred_element_type=jnp.float32)


def dot_t(a, b):
    return lax.dot_general(a, b, (((0,), (0,)), ((), ())), preferred_element_type=jnp.float32)


class Exchange:
    def __init__(self, me, src, dst, relay, send_sem, relay_sem, recv_sem, spare):
        self.me, self.src, self.dst, self.relay = me, src, dst, relay
        self.send_sem, self.relay_sem, self.recv_sem, self.spare = send_sem, relay_sem, recv_sem, spare

    def sign(self, s, upstream):
        return s if s else 1 - 2 * mod(self.me - upstream, 2)

    def copy(self, src, dst, recv_sem, target):
        return pltpu.make_async_remote_copy(
            src_ref=src, dst_ref=dst, send_sem=self.send_sem, recv_sem=recv_sem,
            device_id={"gz": target}, device_id_type=MESH)

    def send(self, routes):
        for d, s in routes:
            sg = self.sign(s, 0)
            src = self.src.at[mod(self.me + sg * d, NZ)]
            target = mod(self.me + sg * (REACH if d > DIRECT else d), NZ)
            if d > DIRECT:
                i = FAR.index((d, s))
                self.copy(src, self.relay.at[i], self.relay_sem.at[i], target).start()
            else:
                self.copy(src, self.dst.at[self.me], self.recv_sem, target).start()

    def forward(self, routes):
        for d, s in routes:
            i = FAR.index((d, s))
            sg = self.sign(s, REACH)
            held = self.relay.at[i]
            pltpu.make_async_copy(held, held, self.relay_sem.at[i]).wait()
            target = mod(self.me + sg * (d - REACH), NZ)
            self.copy(held, self.dst.at[mod(self.me - sg * REACH, NZ)], self.recv_sem, target).start()

    def keep_own(self):
        self.dst[self.me] = self.src[self.me]

    def arrive(self):
        got = self.spare.at[pl.ds(0, NZ - 1)]
        pltpu.make_async_copy(got, got, self.recv_sem).wait()

    def finish(self):
        sent = self.spare.at[pl.ds(0, len(ROUTES) + len(FAR))]
        pltpu.make_async_copy(sent, sent, self.send_sem).wait()


def kernel(resid_hbm, basis_hbm, factor_hbm, coarse_hbm, owner_hbm, out_ref,
           resid, basis, factor, coarse, coarse_t, owner, pick, spread, primal, extra, dual, dual_in, solved, above,
           pack, vec, sol, back, relay, spare, load_sem, send_sem, relay_sem, recv_sem, halo_send, halo_recv):
    gx, gy, gz = lax.axis_index("gx"), lax.axis_index("gy"), lax.axis_index("gz")
    axes = (("gx", gx), ("gy", gy), ("gz", gz))
    sizes = {name: lax.axis_size(name) for name, _ in axes}
    barrier = pltpu.get_barrier_semaphore()
    peers = [{name: mod(at + s, sizes[name])} for name, at in axes for s in (1, -1)]
    peers += [{"gz": mod(gz + s * h, NZ)} for h in range(2, DIRECT + 1) for s in (1, -1)]

    for peer in peers:
        pl.semaphore_signal(barrier, inc=1, device_id=peer, device_id_type=MESH)

    loads = [pltpu.make_async_copy(owner_hbm, owner, load_sem.at[0])]
    for src, dst in ((basis_hbm, basis), (resid_hbm, resid)):
        for f in range(3):
            loads.append(pltpu.make_async_copy(src.at[f], dst.at[f], load_sem.at[len(loads)]))
    for src, dst in ((factor_hbm, factor), (coarse_hbm, coarse)):
        loads.append(pltpu.make_async_copy(src, dst, load_sem.at[len(loads)]))
    for copy in loads:
        copy.start()

    def chunk(ch):
        return slice(ch * LANES, (ch + 1) * LANES)

    def slots():
        loads[0].wait()
        lane = lax.broadcasted_iota(jnp.int32, (1, ITEMS * GROUP), 1)
        item = lane // GROUP
        owners = [owner[i] for i in range(ITEMS)]
        mine = jnp.zeros_like(lane)
        for i in range(ITEMS):
            mine = jnp.where(item == i, owners[i], mine)
        rank = jnp.zeros_like(lane)
        for i in range(ITEMS):
            rank = rank + jnp.where((mine == owners[i]) & (item > i), 1, 0)
        place = (mine * CAP + rank) * GROUP + lax.rem(lane, GROUP)
        rows = lax.broadcasted_iota(jnp.int32, (NZ * BLOCK, ITEMS * GROUP), 0)
        pick[...] = jnp.where(rows == place, 1.0, 0.0).astype(jnp.bfloat16)

    def primal_rows(ch):
        for f in range(3):
            if ch == 0:
                loads[1 + f].wait()
                loads[4 + f].wait()
            t = dot_t(basis[f, :, :PF], resid[f, :, chunk(ch)])
            primal[f * PF:(f + 1) * PF, chunk(ch)] = t.astype(jnp.bfloat16)

    def pack_slots(ch):
        packed = dot(pick[...], primal[:, chunk(ch)]).astype(jnp.bfloat16)
        pack[ch] = packed.reshape(NZ, BLOCK, LANES)

    def dual_rows():
        for f in range(3):
            dual[f] = dot_t(basis[f, :, PF:], resid[f]).astype(jnp.bfloat16)

    def halo(src, dst, step, which):
        for k, (name, at) in enumerate(axes):
            pltpu.make_async_remote_copy(
                src_ref=src.at[k], dst_ref=dst.at[k], send_sem=halo_send.at[which], recv_sem=halo_recv.at[which],
                device_id={name: mod(at + step, sizes[name])}, device_id_type=MESH).start()

    def halo_wait(ref, sem):
        pltpu.make_async_copy(ref, ref, sem).wait()

    def solve():
        halo_wait(dual_in, halo_recv.at[0])
        loads[7].wait()
        halves = [(part[...] * 0.5).reshape(3 * PF, 2 * LANES) for part in (dual_in, dual)]
        load = jnp.concatenate(halves, axis=0).astype(jnp.bfloat16)
        half = dot_t(factor[...], load).astype(jnp.bfloat16)
        solved[...] = dot(factor[...], half).astype(jnp.bfloat16).reshape(6, PF, 2 * LANES)

    def mean():
        halo_wait(above, halo_recv.at[1])
        for k in range(3):
            half_sum = 0.5 * (solved[3 + k].astype(jnp.float32) + above[k].astype(jnp.float32))
            extra[k * 2 * PF:(k + 1) * 2 * PF, :] = dot(basis[k, :, PF:], half_sum.astype(jnp.bfloat16))

    def spread_basis():
        for f in range(3):
            columns = dot_nt(basis[f, :, :PF], pick[:, f * PF:(f + 1) * PF])
            spread[f * 2 * PF:(f + 1) * 2 * PF, :] = columns.astype(jnp.bfloat16)

    def ctrans():
        loads[8].wait()
        coarse_t[...] = coarse[...].T

    def exchange(which, ch, src, dst):
        return Exchange(gz, src.at[ch], dst.at[ch], relay.at[which, ch], send_sem.at[which, ch],
                        relay_sem.at[which, ch], recv_sem.at[which, ch], spare)

    trips = {("F", ch): exchange(0, ch, pack, vec) for ch in range(2)}
    trips |= {("B", ch): exchange(1, ch, sol, back) for ch in range(2)}

    def coarse_apply(ch):
        trips["F", ch].arrive()
        answer = dot(coarse_t[...], vec[ch].reshape(NZ * BLOCK, LANES)).astype(jnp.bfloat16)
        sol[ch] = answer.reshape(NZ, BLOCK, LANES)
        trips["B", ch].keep_own()

    def final(ch):
        trips["B", ch].arrive()
        total = dot(spread[...], back[ch].reshape(NZ * BLOCK, LANES)) + extra[:, chunk(ch)]
        out_ref[:, :, chunk(ch)] = total.astype(jnp.bfloat16).reshape(3, 2 * PF, LANES)

    run = {
        "slots": slots,
        "barrier": lambda: pl.semaphore_wait(barrier, len(peers)),
        "dual": dual_rows,
        "up": lambda: halo(dual, dual_in, 1, 0),
        "solve": solve,
        "down": lambda: halo(solved, above, -1, 1),
        "mean": mean,
        "ctrans": ctrans,
        "spread": spread_basis,
    }
    for ch in range(2):
        run[f"primal{ch}"] = functools.partial(primal_rows, ch)
        run[f"pack{ch}"] = functools.partial(pack_slots, ch)
        run[f"keep{ch}"] = trips["F", ch].keep_own
        run[f"coarse{ch}"] = functools.partial(coarse_apply, ch)
        run[f"final{ch}"] = functools.partial(final, ch)
        for way in "FB":
            trip = trips[way, ch]
            run[f"{way}{ch}far"] = functools.partial(trip.send, FAR)
            run[f"{way}{ch}near"] = functools.partial(trip.send, NEAR)
            run[f"{way}{ch}n43"] = functools.partial(trip.send, NEAR[:4])
            run[f"{way}{ch}n21"] = functools.partial(trip.send, NEAR[4:])
            run[f"{way}{ch}fwd"] = functools.partial(trip.forward, FAR)
            run[f"{way}{ch}fwA"] = functools.partial(trip.forward, FAR[:3])
            run[f"{way}{ch}fwB"] = functools.partial(trip.forward, FAR[3:])
    for step in STEPS:
        with jax.named_scope(step):
            run[step]()
    for trip in trips.values():
        trip.finish()
    halo_wait(dual_in, halo_send.at[0])
    halo_wait(above, halo_send.at[1])


def body(residual, face_basis, factor, coarse_inv, item_owner):
    bf16 = jnp.bfloat16
    blocks = pltpu.VMEM((2, NZ, BLOCK, LANES), bf16)
    faces = pltpu.VMEM((3, 2 * PF, 2 * LANES), bf16)
    halves = pltpu.VMEM((3, PF, 2 * LANES), bf16)
    square = pltpu.VMEM((NZ * BLOCK, NZ * BLOCK), bf16)
    table = pltpu.SMEM((ITEMS,), jnp.int32)
    semaphores = pltpu.SemaphoreType.DMA
    result = pl.pallas_call(
        kernel,
        out_shape=pltpu.VMEM((3, 2 * PF, 2 * LANES), bf16),
        in_specs=[pl.BlockSpec(memory_space=pltpu.HBM)] * 5,
        out_specs=pl.BlockSpec(memory_space=pltpu.VMEM),
        scratch_shapes=[
            faces, faces, square, square, square, table,
            pltpu.VMEM((NZ * BLOCK, ITEMS * GROUP), bf16), square,
            pltpu.VMEM((ITEMS * GROUP, 2 * LANES), bf16),
            pltpu.VMEM((NZ * BLOCK, 2 * LANES), jnp.float32),
            halves, halves, pltpu.VMEM((6, PF, 2 * LANES), bf16), halves,
            blocks, blocks, blocks, blocks,
            pltpu.VMEM((2, 2, len(FAR), BLOCK, LANES), bf16),
            pltpu.VMEM((len(ROUTES) + len(FAR), BLOCK, LANES), bf16),
            semaphores((9,)),
            semaphores((2, 2)), semaphores((2, 2, len(FAR))), semaphores((2, 2)), semaphores((2,)), semaphores((2,)),
        ],
        compiler_params=pltpu.CompilerParams(collective_id=0, has_side_effects=True, vmem_limit_bytes=60 * 1024 * 1024),
    )(residual[0, 0, 0], face_basis[0, 0, 0], factor[0, 0, 0], coarse_inv[0, 0, 0], item_owner[0, 0, 0])
    return result[None, None, None]


def solution(mesh):
    in_specs = (
        P("gx", "gy", "gz", None, None, None),
        P("gx", "gy", "gz", None, None, None),
        P("gx", "gy", "gz", None, None),
        P("gx", "gy", "gz", None, None),
        P("gx", "gy", "gz", None),
    )
    out_specs = P("gx", "gy", "gz", None, None, None)
    return jax.shard_map(body, mesh=mesh, in_specs=in_specs, out_specs=out_specs, check_vma=False)
```

time: 78.6 us -> 51.5 us (0.66)
  Pallas kernels: 0 us -> 50.6 us
  starting transfers between devices: 37 us -> 0 us
  waiting for transfers between devices: 27.1 us -> 0 us
  local copies, waits for them, and re-layouts: 7.96 us -> 0.75 us
  matrix products: 5.16 us -> 0 us
    pallas_call x0 -> x1, Pallas kernels: none -> 50.6 us  [body(): pl.pallas_call(kernel, out_shape=pltpu.VMEM((3, 2 * PF, 2 * LANES), bf16)...]
    all_to_all x2 -> x0, waiting for transfers between devices: 21.5 us -> none  [the longest x1 18.4 us: body(): lax.all_to_all(outgoing, 'gz', split_axis=0, concat_axis=0, tiled=True)]
    all_to_all x2 -> x0, starting transfers between devices: 19.7 us -> none  [the longest x1 15.2 us: body(): lax.all_to_all(outgoing, 'gz', split_axis=0, concat_axis=0, tiled=True)]
    ppermute x6 -> x0, starting transfers between devices: 17.3 us -> none  [shifted(): return lax.ppermute(block, axis, route)]
    ppermute x6 -> x0, waiting for transfers between devices: 5.67 us -> none  [shifted(): return lax.ppermute(block, axis, route)]
    dot_general x4 -> x0, matrix products: 5.16 us -> none  [the longest x1 2.82 us: body(): jnp.dot(local_factor, half_solve, preferred_element_type=jnp.float32)]
    scatter x1 -> x0, local copies, waits for them, and re-layouts: 3.88 us -> none  [body(): outgoing.at[send_slot].set(primal_items)]
    broadcast_in_dim x4 -> x0, local copies, waits for them, and re-layouts: 1.86 us -> none  [the longest x1 0.92 us: body(): return result.astype(jnp.bfloat16)[None, None, None]]
  transfers between devices with their start and end apart: 8 -> 0, of which waited for: 3 -> 0; matrix products, arithmetic and copies ran while one was open for 7% -> 0% of each run, Pallas kernels for 0% -> 0%
where the time goes in v1:
time: 51.5 us; the launch traced here: 51.3 us
  Pallas kernels  50.6 us (98%)
  local copies, waits for them, and re-layouts  0.75 us (1%)
    pallas_call x1, Pallas kernels, body(): pl.pallas_call(kernel, out_shape=pltpu.VMEM((3, 2 * PF, 2 * LANES), bf16)...  50.6 us

profile of v1, /device:TPU:6, one launch (start us, length us, event | category | flops | bytes accessed | tf_op | source)
XLA Modules:
  0.0 51.3 jit_solution(10640971021729569469)
XLA Ops:
  0.0 50.6 %shard_map.55 = bf16[3,256,256]{2,1,0:T(8,128)(2,1)S(1)} custom-call(bf16[3,256,256]{2,1,0:T(8,128)(2,1)} %bitcast.9, bf16[3,256,256]{2,1,0:T(8,128)(2,1)} %bitcast.10, bf16[768,768]{1,0:T(8,128)(2,1)} %bitcast.7, bf16[768,768]{1,0:T(8,128)(2,1)} %bitcast.8, s32[24]{0:T(128)} %bitcast.11), custom_call_target="tpu_custom_call" | custom-call | tf_op jit(solution)/shard_map/pallas_call | solution.py:271
  50.6 0.7 %copy.7 = bf16[1,1,1,3,256,256]{5,4,3,2,1,0:T(8,128)(2,1)} copy(bf16[1,1,1,3,256,256]{5,4,3,2,1,0:T(8,128)(2,1)S(1)} %bitcast.6) | data formatting | bytes 786432

commit v2 on v1

--- a/solution.py
+++ b/solution.py
@@ -15,8 +15,8 @@
 NZ = 16
 LANES = 128
 BLOCK = CAP * GROUP
-REACH = 4
 DIRECT = 4
+LEG = {8: 4, 7: 4, 6: 3, 5: 3}
 
 FAR = [(8, 0)] + [(d, s) for d in range(7, DIRECT, -1) for s in (1, -1)]
 NEAR = [(d, s) for d in range(DIRECT, 0, -1) for s in (1, -1)]
@@ -37,8 +37,10 @@
     "F1far",
     "keep1",
     "spread",
-    "F0fwd",
-    "F1near",
+    "F0fwA",
+    "F1n43",
+    "F0fwB",
+    "F1n21",
     "solve",
     "down",
     "ctrans",
@@ -51,8 +53,9 @@
     "B1far",
     "B0fwd",
     "B1n43",
-    "B1fwd",
+    "B1fwA",
     "B1n21",
+    "B1fwB",
     "final0",
     "final1",
 )
@@ -91,7 +94,7 @@
         for d, s in routes:
             sg = self.sign(s, 0)
             src = self.src.at[mod(self.me + sg * d, NZ)]
-            target = mod(self.me + sg * (REACH if d > DIRECT else d), NZ)
+            target = mod(self.me + sg * (LEG[d] if d > DIRECT else d), NZ)
             if d > DIRECT:
                 i = FAR.index((d, s))
                 self.copy(src, self.relay.at[i], self.relay_sem.at[i], target).start()
@@ -101,11 +104,11 @@
     def forward(self, routes):
         for d, s in routes:
             i = FAR.index((d, s))
-            sg = self.sign(s, REACH)
+            sg = self.sign(s, LEG[d])
             held = self.relay.at[i]
             pltpu.make_async_copy(held, held, self.relay_sem.at[i]).wait()
-            target = mod(self.me + sg * (d - REACH), NZ)
-            self.copy(held, self.dst.at[mod(self.me - sg * REACH, NZ)], self.recv_sem, target).start()
+            target = mod(self.me + sg * (d - LEG[d]), NZ)
+            self.copy(held, self.dst.at[mod(self.me - sg * LEG[d], NZ)], self.recv_sem, target).start()
 
     def keep_own(self):
         self.dst[self.me] = self.src[self.me]
@@ -126,9 +129,8 @@
     axes = (("gx", gx), ("gy", gy), ("gz", gz))
     sizes = {name: lax.axis_size(name) for name, _ in axes}
     barrier = pltpu.get_barrier_semaphore()
-    peers = [{name: mod(at + s, sizes[name])} for name, at in axes for s in (1, -1)]
-    peers += [{"gz": mod(gz + s * h, NZ)} for h in range(2, DIRECT + 1) for s in (1, -1)]
-
+    peers = [{"gz": mod(gz + s * h, NZ)} for h in range(DIRECT, 1, -1) for s in (1, -1)]
+    peers += [{name: mod(at + s, sizes[name])} for name, at in axes[::-1] for s in (1, -1)]
     for peer in peers:
         pl.semaphore_signal(barrier, inc=1, device_id=peer, device_id_type=MESH)
 

time: 51.5 us -> 51.5 us (level)
  no operation moved by 1% of the time
where the time goes in v2:
time: 51.5 us; the launch traced here: 51.3 us
  Pallas kernels  50.6 us (98%)
  local copies, waits for them, and re-layouts  0.75 us (1%)
    pallas_call x1, Pallas kernels, body(): pl.pallas_call(kernel, out_shape=pltpu.VMEM((3, 2 * PF, 2 * LANES), bf16)...  50.6 us

profile of v2, /device:TPU:6, one launch (start us, length us, event | category | flops | bytes accessed | tf_op | source)
XLA Modules:
  0.0 51.3 jit_solution(16677288289163951052)
XLA Ops:
  0.0 50.6 %shard_map.55 = bf16[3,256,256]{2,1,0:T(8,128)(2,1)S(1)} custom-call(bf16[3,256,256]{2,1,0:T(8,128)(2,1)} %bitcast.9, bf16[3,256,256]{2,1,0:T(8,128)(2,1)} %bitcast.10, bf16[768,768]{1,0:T(8,128)(2,1)} %bitcast.7, bf16[768,768]{1,0:T(8,128)(2,1)} %bitcast.8, s32[24]{0:T(128)} %bitcast.11), custom_call_target="tpu_custom_call" | custom-call | tf_op jit(solution)/shard_map/pallas_call | solution.py:273
  50.6 0.7 %copy.7 = bf16[1,1,1,3,256,256]{5,4,3,2,1,0:T(8,128)(2,1)} copy(bf16[1,1,1,3,256,256]{5,4,3,2,1,0:T(8,128)(2,1)S(1)} %bitcast.6) | data formatting | bytes 786432
